TPU v7x, 512 devices: a whole 4x4x16 slice. The times are simulated.
512 devices in a mesh: tile: 32 (over x, y, core), mem: 16 (over z).
Axes of the slice: x: 4, y: 4, z: 16, core: 2. Of those that a mesh axis runs over, the one named last changes fastest.
Arguments:
- velocity: bfloat16 [96, 2, 8, 131072], P('mem', None, None, 'tile'), may hold values from -6 to 6
- start_frac: float32 [2, 65536], P(None, 'tile'), may hold values from 0 to 1
- observed: float32 [2, 65536], P(None, 'tile'), may hold values from -0.5 to 1.5
- obs_sd: float32 [65536], P('tile'), may hold values from 0.3 to 3
- tile_of: int32 [65536, 1], P('tile'), may hold values from 0 to 31; in each aligned block of 2048 rows (0 to 2047, 2048 to 4095, ...) at most 128 rows name the same one
- cell_of: int32 [65536], P('tile'), may hold values from 0 to 4030, as said below
Outputs:
- analysis_velocity: bfloat16 [96, 2, 8, 131072], P('mem', None, None, 'tile')
- analysis_positions: float32 [96, 2, 65536], P('mem', None, 'tile')
Inputs may be any that keep to these rules, and one draw needn't show every extreme that they name: cell_of is i * 64 + j with i and j below 63, so the stencil's four cells lie in the same tile. `tile_of`: of the drifters of one index of tile, at most 128 name one tile, a bound that some block reaches of them.
All inputs are finite; a program needn't handle non-finite values.
Results may differ from a plain program's by a relative error of at most 0.0048.
Values may be sent and summed in bfloat16 or wider, within the bound.
A program may use at most 64 MiB of HBM per device.

v0:
```python
import functools

import jax
import jax.numpy as jnp
from jax import lax
from jax.experimental import pallas as pl
from jax.experimental.pallas import tpu as pltpu
from jax.sharding import PartitionSpec as P

BX = 64
LANES = 128
LOW = 256
STEP = 0.2
MESH = pl.DeviceIdType.MESH
HIGHEST = lax.Precision.HIGHEST
BF = jnp.bfloat16
F32 = jnp.float32


def three_parts(x):
    high = x.astype(BF).astype(F32)
    rest = x - high
    middle = rest.astype(BF).astype(F32)
    return high, middle, rest - middle


def nt_dot(a, b, precision=None):
    return lax.dot_general(
        a, b, (((1,), (1,)), ((), ())), precision=precision, preferred_element_type=F32
    )


def bilinear(corner, x, y):
    return (
        (1.0 - x) * (1.0 - y) * corner[0]
        + x * (1.0 - y) * corner[1]
        + (1.0 - x) * y * corner[2]
        + x * y * corner[3]
    )


def remote(src, dst, send_sem, recv_sem, axis, peer):
    return pltpu.make_async_remote_copy(
        src_ref=src,
        dst_ref=dst,
        send_sem=send_sem,
        recv_sem=recv_sem,
        device_id={axis: peer},
        device_id_type=MESH,
    )


def gram_kernel(
    tiles,
    planes,
    local_members,
    dest_ref,
    cell_ref,
    frac_ref,
    obs_ref,
    sd_ref,
    table_ref,
    all_out,
    gram_out,
    slot_ref,
    req,
    asked,
    pred,
    ret,
    parts,
    zsend,
    zall,
    gsend,
    grecv,
    gpart,
    gplane,
    gall,
    send_a,
    send_b,
    send_z,
    recv_a,
    recv_b,
    recv_c,
    recv_e,
):
    me = lax.axis_index("tile")
    mz = lax.axis_index("mem")
    drifters = dest_ref.shape[1]
    width = min(256, drifters)
    members = planes * local_members
    rows = planes * 8

    barrier = pltpu.get_barrier_semaphore()

    def greet_tile(i, carry):
        pl.semaphore_signal(
            barrier, inc=1, device_id={"tile": lax.rem(me + i, tiles)}, device_id_type=MESH
        )
        return carry

    def greet_mem(i, carry):
        pl.semaphore_signal(
            barrier, inc=1, device_id={"mem": lax.rem(mz + i, planes)}, device_id_type=MESH
        )
        return carry

    lax.fori_loop(1, tiles, greet_tile, 0)
    lax.fori_loop(1, planes, greet_mem, 0)

    tile_row = lax.broadcasted_iota(jnp.int32, (tiles, width), 0)
    earlier = (
        lax.broadcasted_iota(jnp.int32, (width, width), 0)
        < lax.broadcasted_iota(jnp.int32, (width, width), 1)
    ).astype(F32).astype(BF)
    count = jnp.zeros((tiles, 1), F32)
    for b in range(drifters // width):
        lanes = pl.ds(b * width, width)
        hot = (tile_row == dest_ref[:, lanes]).astype(F32)
        before = jnp.dot(hot.astype(BF), earlier, preferred_element_type=F32) + count
        slot_ref[:, lanes] = jnp.sum(hot * before, axis=0, keepdims=True)
        count = count + jnp.sum(hot, axis=1, keepdims=True)

    total = jnp.zeros((tiles * 8, LANES), F32)
    for b in range(drifters // width):
        lanes = pl.ds(b * width, width)
        cell = cell_ref[:, lanes]
        values = [(cell >> 8).astype(F32), (cell & (LOW - 1)).astype(F32)]
        values += three_parts(frac_ref[0:1, lanes]) + three_parts(frac_ref[1:2, lanes])
        row = lax.broadcasted_iota(jnp.int32, (8, width), 0)
        block = jnp.broadcast_to(values[7], (8, width))
        for v in range(7):
            block = jnp.where(row == v, values[v], block)
        tile_index = lax.broadcasted_iota(jnp.int32, (tiles, 8, width), 0)
        spread = jnp.where(tile_index == dest_ref[:, lanes][None], block[None], 0.0)
        spread = spread.reshape(tiles * 8, width).astype(BF)
        slot_row = lax.broadcasted_iota(jnp.int32, (LANES, width), 0).astype(F32)
        hot_slot = (slot_row == slot_ref[:, lanes]).astype(F32).astype(BF)
        total = total + nt_dot(spread, hot_slot)
    req[...] = total.reshape(tiles, 8, LANES)

    pl.semaphore_wait(barrier, tiles + planes - 2)

    def ask(i, carry):
        peer = lax.rem(me + i, tiles)
        remote(
            req.at[peer], asked.at[me], send_a.at[peer], recv_a.at[me], "tile", peer
        ).start()
        return carry

    lax.fori_loop(1, tiles, ask, 0)
    asked[me] = req[me]

    def serve(i, carry):
        src = lax.rem(me + tiles - i, tiles)

        @pl.when(i > 0)
        def _():
            remote(
                req.at[src], asked.at[src], send_a.at[src], recv_a.at[src], "tile", src
            ).wait_recv()

        block = asked[src]
        high, low = block[0:1], block[1:2]
        start_x = block[2:3] + block[3:4] + block[4:5]
        start_y = block[5:6] + block[6:7] + block[7:8]
        lows, highs = [], []
        for shift in (0, 1, BX, BX + 1):
            moved = low + float(shift)
            over = moved >= float(LOW)
            lows.append(jnp.where(over, moved - float(LOW), moved))
            highs.append(jnp.where(over, high + 1.0, high))
        low4 = jnp.concatenate(lows, axis=1)
        high4 = jnp.concatenate(highs, axis=1)
        cell_row = lax.broadcasted_iota(jnp.int32, (LOW, 4 * LANES), 0).astype(F32)
        hot = (cell_row == low4).astype(F32).astype(BF)
        found = jnp.dot(table_ref[...], hot, preferred_element_type=F32)
        picked = found[0:16]
        for h in range(1, table_ref.shape[0] // 16):
            picked = jnp.where(high4 == float(h), found[16 * h : 16 * h + 16], picked)
        corner_x = [picked[0:8, LANES * q : LANES * (q + 1)] for q in range(4)]
        corner_y = [picked[8:16, LANES * q : LANES * (q + 1)] for q in range(4)]
        x = jnp.broadcast_to(start_x, (8, LANES))
        y = jnp.broadcast_to(start_y, (8, LANES))
        for _ in range(2):
            half_x = x + 0.5 * STEP * bilinear(corner_x, x, y)
            half_y = y + 0.5 * STEP * bilinear(corner_y, x, y)
            x, y = (
                x + STEP * bilinear(corner_x, half_x, half_y),
                y + STEP * bilinear(corner_y, half_x, half_y),
            )
        pred[src, 0] = x
        pred[src, 1] = y

        @pl.when(i > 0)
        def _():
            remote(
                pred.at[src], ret.at[me], send_b.at[src], recv_b.at[me], "tile", src
            ).start()

        @pl.when(i == 0)
        def _():
            ret[src, 0] = x
            ret[src, 1] = y

        return carry

    lax.fori_loop(0, tiles, serve, 0)

    def asked_sent(i, carry):
        peer = lax.rem(me + i, tiles)
        remote(
            req.at[peer], asked.at[me], send_a.at[peer], recv_a.at[me], "tile", peer
        ).wait_send()
        return carry

    lax.fori_loop(1, tiles, asked_sent, 0)

    def returned(i, carry):
        peer = lax.rem(me + i, tiles)
        copy = remote(pred.at[peer], ret.at[peer], send_b.at[peer], recv_b.at[peer], "tile", peer)
        copy.wait_send()
        copy.wait_recv()
        return carry

    lax.fori_loop(1, tiles, returned, 0)

    for k, part in enumerate(three_parts(ret[...].reshape(tiles * 16, LANES))):
        parts[:, LANES * k : LANES * (k + 1)] = part.astype(BF)
    shares = width // LANES

    def order(i, carry):
        lanes = pl.ds(pl.multiple_of(i * width, width), width)
        slot_row = lax.broadcasted_iota(jnp.int32, (LANES, width), 0).astype(F32)
        hot = (slot_row == slot_ref[:, lanes]).astype(F32).astype(BF)
        hot = jnp.concatenate([hot, hot, hot], axis=0)
        found = jnp.dot(parts[...], hot, preferred_element_type=F32)
        dest = dest_ref[:, lanes]
        picked = found[0:16]
        for t in range(1, tiles):
            picked = jnp.where(dest == t, found[16 * t : 16 * t + 16], picked)
        for s in range(shares):
            zsend[i * shares + s, 0] = picked[0:8, LANES * s : LANES * (s + 1)]
            zsend[i * shares + s, 1] = picked[8:16, LANES * s : LANES * (s + 1)]
        return carry

    lax.fori_loop(0, drifters // width, order, 0)

    def share(i, carry):
        peer = lax.rem(mz + i, planes)
        remote(zsend.at[peer], zall.at[mz], send_z.at[peer], recv_c.at[mz], "mem", peer).start()
        return carry

    lax.fori_loop(1, planes, share, 0)
    zall[mz] = zsend[mz]

    def shared(i, carry):
        peer = lax.rem(mz + i, planes)
        copy = remote(zsend.at[peer], zall.at[peer], send_z.at[peer], recv_c.at[peer], "mem", peer)
        copy.wait_send()
        copy.wait_recv()
        return carry

    lax.fori_loop(1, planes, shared, 0)

    row = lax.broadcasted_iota(jnp.int32, (rows, LANES), 0)
    real = (row & 7) < local_members
    own = pl.ds(pl.multiple_of(mz * LANES, LANES), LANES)
    sd = sd_ref[:, own]
    inverse_scale = 1.0 / (sd * jnp.sqrt(jnp.full(sd.shape, members - 1, F32)))
    gram = jnp.zeros((rows, rows), F32)
    for c in range(2):
        p = zall[:, c].reshape(rows, LANES)
        mean = jnp.sum(jnp.where(real, p, 0.0), axis=0, keepdims=True) * (1.0 / members)
        anomaly = jnp.where(real, (p - mean) * inverse_scale, 0.0)
        innovation = (obs_ref[c : c + 1, own] - mean) / sd
        left = jnp.where(row == local_members, innovation, anomaly)
        gram = gram + nt_dot(left, anomaly, HIGHEST)
    chunk = rows // tiles
    for t in range(tiles):
        gsend[t] = gram[chunk * t : chunk * (t + 1)]

    def scatter(i, carry):
        peer = lax.rem(me + i, tiles)
        remote(gsend.at[peer], grecv.at[me], send_a.at[peer], recv_a.at[me], "tile", peer).start()
        return carry

    lax.fori_loop(1, tiles, scatter, 0)
    grecv[me] = gsend[me]

    def scattered(i, carry):
        peer = lax.rem(me + i, tiles)
        copy = remote(
            gsend.at[peer], grecv.at[peer], send_a.at[peer], recv_a.at[peer], "tile", peer
        )
        copy.wait_send()
        copy.wait_recv()
        return carry

    lax.fori_loop(1, tiles, scattered, 0)
    partial = grecv[0]
    for t in range(1, tiles):
        partial = partial + grecv[t]
    gpart[...] = partial

    def plane(i, carry):
        peer = lax.rem(mz + i, planes)
        remote(gpart, gplane.at[mz], send_z.at[peer], recv_e.at[mz], "mem", peer).start()
        return carry

    lax.fori_loop(1, planes, plane, 0)
    gplane[mz] = partial

    def planed(i, carry):
        peer = lax.rem(mz + i, planes)
        copy = remote(gpart, gplane.at[peer], send_z.at[peer], recv_e.at[peer], "mem", peer)
        copy.wait_send()
        copy.wait_recv()
        return carry

    lax.fori_loop(1, planes, planed, 0)
    summed = gplane[0]
    for z in range(1, planes):
        summed = summed + gplane[z]
    gpart[...] = summed

    def gather(i, carry):
        peer = lax.rem(me + i, tiles)
        remote(gpart, gall.at[me], send_b.at[peer], recv_b.at[me], "tile", peer).start()
        return carry

    lax.fori_loop(1, tiles, gather, 0)
    gall[me] = summed

    def gathered(i, carry):
        peer = lax.rem(me + i, tiles)
        copy = remote(gpart, gall.at[peer], send_b.at[peer], recv_b.at[peer], "tile", peer)
        copy.wait_send()
        copy.wait_recv()
        return carry

    lax.fori_loop(1, tiles, gathered, 0)
    all_out[...] = zall[...]
    gram_out[...] = gall[...]


def gram_of_all(tiles, planes, local_members, dest, cell, frac, obs, sd, table):
    rows = planes * 8
    chunk = rows // tiles
    vmem = pl.BlockSpec(memory_space=pltpu.VMEM)
    dma = pltpu.SemaphoreType.DMA
    f32 = lambda *shape: pltpu.VMEM(shape, F32)
    return pl.pallas_call(
        functools.partial(gram_kernel, tiles, planes, local_members),
        out_shape=(
            jax.ShapeDtypeStruct((planes, 2, 8, LANES), F32),
            jax.ShapeDtypeStruct((tiles, chunk, rows), F32),
        ),
        in_specs=[vmem] * 6,
        out_specs=(vmem, vmem),
        scratch_shapes=[
            f32(1, dest.shape[1]),
            f32(tiles, 8, LANES),
            f32(tiles, 8, LANES),
            f32(tiles, 2, 8, LANES),
            f32(tiles, 2, 8, LANES),
            pltpu.VMEM((tiles * 16, 3 * LANES), BF),
            f32(planes, 2, 8, LANES),
            f32(planes, 2, 8, LANES),
            f32(tiles, chunk, rows),
            f32(tiles, chunk, rows),
            f32(chunk, rows),
            f32(planes, chunk, rows),
            f32(tiles, chunk, rows),
            dma((tiles,)),
            dma((tiles,)),
            dma((planes,)),
            dma((tiles,)),
            dma((tiles,)),
            dma((planes,)),
            dma((planes,)),
        ],
        compiler_params=pltpu.CompilerParams(collective_id=0, has_side_effects=True),
        cost_estimate=pl.CostEstimate(
            flops=100_000_000_000, bytes_accessed=4_000_000, transcendentals=0
        ),
        name="gram",
    )(dest, cell, frac, obs, sd, table)


def combine_kernel(weight_ref, field_ref, *refs):
    out_ref = refs[-1]
    rows = weight_ref.shape[1]
    width = field_ref.shape[2]
    field = field_ref[...].reshape(rows, width)
    out = jnp.dot(weight_ref[...], field, preferred_element_type=F32)
    out_ref[...] = out.astype(BF).reshape(out_ref.shape)


def combine(kron, gathered, first, cells, width, so_far):
    members, layers, part = gathered.shape
    local = kron.shape[0] // layers
    start = first // width
    ins = [
        pl.BlockSpec(kron.shape, lambda i: (0, 0)),
        pl.BlockSpec((members, layers, width), lambda i: (0, 0, i)),
    ]
    args = [kron, gathered]
    alias = {}
    if so_far is not None:
        ins.append(pl.BlockSpec(memory_space=pl.ANY))
        args.append(so_far)
        alias = {2: 0}
    return pl.pallas_call(
        combine_kernel,
        grid=(part // width,),
        in_specs=ins,
        out_specs=pl.BlockSpec((local, layers, width), lambda i: (0, 0, start + i)),
        out_shape=jax.ShapeDtypeStruct((local, layers, cells), BF),
        input_output_aliases=alias,
        cost_estimate=pl.CostEstimate(
            flops=2 * members * local * layers * part,
            bytes_accessed=2 * members * layers * part,
            transcendentals=0,
        ),
        name="combine",
    )(*args)


def ensemble_weights(gram_matrix, projection):
    members = gram_matrix.shape[0]
    identity = jnp.eye(members, dtype=jnp.float32)
    factor = jnp.linalg.cholesky(identity + gram_matrix)
    inverse_root = lax.linalg.triangular_solve(
        factor, identity, left_side=True, lower=True, transpose_a=True
    )
    half_solve = jnp.dot(projection[None], inverse_root, precision=HIGHEST)
    mean_weight = jnp.sum(inverse_root * half_solve, axis=1, keepdims=True)
    combined = mean_weight + jnp.sqrt(jnp.float32(members - 1)) * inverse_root
    return combined - jnp.mean(combined, axis=0, keepdims=True) + 1.0 / members


CHUNKS = (3072, 1024)


def shards(velocity, start_frac, observed, obs_sd, tile_of, cell_of):
    local, comps, levels, cells = velocity.shape
    tiles = lax.axis_size("tile")
    planes = lax.axis_size("mem")
    members = planes * local
    drifters = cell_of.shape[0]
    layers = comps * levels

    field = velocity.reshape(local, layers, cells)
    gathered, first = [], 0
    for size in CHUNKS:
        piece = lax.slice_in_dim(field, first, first + size, axis=2)
        gathered.append((first, lax.all_gather(piece, "mem", axis=0, tiled=True)))
        first += size

    table = velocity[:, :, 0, :].reshape(local, comps, cells // LOW, LOW)
    table = jnp.pad(table.transpose(2, 1, 0, 3), ((0, 0), (0, 0), (0, 8 - local), (0, 0)))
    table = table.reshape(-1, LOW)
    predicted, gram = gram_of_all(
        tiles,
        planes,
        local,
        tile_of.reshape(1, drifters),
        cell_of.reshape(1, drifters),
        start_frac,
        observed,
        obs_sd.reshape(1, drifters),
        table,
    )
    gram = gram.reshape(planes, 8, planes, 8)
    projection = gram[0, local, :, :local].reshape(members)
    gram_matrix = gram[:, :local, :, :local].reshape(members, members)
    weights = ensemble_weights(gram_matrix, projection)

    everyone = predicted[:, :, :local]
    moved = jnp.einsum(
        "zmn,zcmp->ncp", weights.reshape(planes, local, members), everyone, precision=HIGHEST
    )
    moved = lax.all_to_all(
        moved.reshape(planes, local, comps, LANES), "mem", split_axis=0, concat_axis=0, tiled=True
    )
    new_positions = moved.transpose(1, 2, 0, 3).reshape(local, comps, drifters)

    first_member = lax.axis_index("mem") * local
    own_columns = lax.dynamic_slice_in_dim(weights, first_member, local, 1).astype(BF)
    same = jnp.eye(layers, dtype=BF)
    kron = own_columns.T[:, None, :, None] * same[None, :, None, :]
    kron = kron.reshape(local * layers, members * layers)
    out = None
    for first, part in gathered:
        out = combine(kron, part, first, cells, 512, out)
    return (out.reshape(local, comps, levels, cells), new_positions)


def solution(mesh):
    in_specs = (
        P("mem", None, None, "tile"),
        P(None, "tile"),
        P(None, "tile"),
        P("tile"),
        P("tile", None),
        P("tile"),
    )
    out_specs = (P("mem", None, None, "tile"), P("mem", None, "tile"))
    return jax.shard_map(shards, mesh=mesh, in_specs=in_specs, out_specs=out_specs, check_vma=False)
```

profile of v0, /device:TPU:2, one launch (start us, length us, event | category | flops | bytes accessed | tf_op | source)
XLA Modules:
  0.0 228.1 jit_solution(9488018609741905218)
XLA Ops:
  7.2 0.0 all-gather.5.cloned.1.call-start
  7.2 1.9 slice.37
  9.1 0.0 all-gather.5.cloned.1.call-update
  9.2 0.0 all-gather.3.cloned.1.call-start
  9.2 1.6 slice.36
  10.8 0.0 all-gather.3.cloned.1.call-update
  10.9 1.7 slice_reduce_fusion
  12.6 0.1 reshape_squeeze.3
  12.6 0.1 copy.39
  12.7 0.7 pad.4.clone
  13.4 68.9 %gram.1 = (f32[16,2,8,128]{3,2,1,0:T(8,128)}, f32[32,4,128]{2,1,0:T(4,128)}) custom-call(s32[1,2048]{1,0:T(1,128)} %bitcast.54, s32[1,2048]{1,0:T(1,128)} %bitcast.55, f32[2,2048]{1,0:T(2,128)} %frac_ref.1, f32[2,2048]{1,0:T(2,128)} %obs_ref.1, f32[1,2048]{1,0:T(1,128)} %bitcast.56, bf16[256,256]{1,0:T(8,128)(2,1)} %bitcast.52), custom_call_target="tpu_custom_call" | custom-call | flops 99999997952 | bytes 4000000 | tf_op jit(solution)/shard_map/gram/pallas_call | solution.py:352
  82.3 1.4 reshape.73
  83.7 0.0 copy-start
  83.7 0.1 slice.34
  83.8 0.4 reshape.74
  84.2 0.1 copy.26
  84.3 8.8 %cholesky.18 = f32[96,96]{1,0:T(8,128)S(1)} custom-call(f32[96,96]{1,0:T(8,128)S(1)} %fusion.5), custom_call_target="Cholesky" | custom-call | tf_op jit(solution)/shard_map/jit(cholesky)/cholesky | solution.py:432
  93.1 0.6 compare_reduce_fusion
  93.8 0.7 fusion.2
  94.4 7.4 %custom-call.6 = f32[1,96,96]{1,2,0:T(8,128)S(1)} custom-call(f32[1,96,96]{2,1,0:T(8,128)S(1)} %fusion.2), custom_call_target="InvertDiagBlocksLowerTriangular" | custom-call | tf_op jit(solution)/shard_map/triangular_solve | solution.py:433
  101.8 0.1 reshape.80
  101.9 0.2 fusion.3
  102.1 0.2 convolution_bitcast_fusion.1
  102.3 0.1 multiply_reduce_fusion
  102.4 0.1 fusion.6
  102.5 0.1 subtract_add_fusion
  102.6 0.1 copy.27
  102.7 0.4 reshape.86
  103.2 0.8 copy.33
  104.0 0.0 copy-done
  104.0 0.4 convolution_bitcast_fusion
  104.5 0.7 copy.31
  105.1 3.5 %all-to-all-start = ((f32[16,6,2,128]{3,2,1,0:T(2,128)}), f32[16,6,2,128]{3,2,1,0:T(2,128)S(1)}, u32[]{:S(2)}, u32[]{:S(2)}) async-start(f32[16,6,2,128]{3,2,1,0:T(2,128)} %copy.31), calls=%async_computation | async-start | bytes 196608 | tf_op jit(solution)/shard_map/all_to_all | solution.py:483
  108.7 0.2 broadcast_multiply_fusion
  108.9 4.5 %mul.42.weight_ref = bf16[96,1536]{1,0:T(8,128)(2,1)} reshape(bf16[6,16,96,16]{3,2,1,0:T(8,128)(2,1)S(1)} %broadcast_multiply_fusion) | data formatting | bytes 589824 | tf_op jit(solution)/shard_map/mul | solution.py:491
  113.5 9.9 %all-to-all-done = f32[16,6,2,128]{3,2,1,0:T(2,128)S(1)} async-done(((f32[16,6,2,128]{3,2,1,0:T(2,128)}), f32[16,6,2,128]{3,2,1,0:T(2,128)S(1)}, u32[]{:S(2)}, u32[]{:S(2)}) %all-to-all-start) | async-done | bytes 98336 | tf_op jit(solution)/shard_map/all_to_all | solution.py:483
  123.4 0.7 copy_bitcast_fusion
  124.0 18.8 %all-gather.5.cloned.1.call-done.field_ref = bf16[96,16,3072]{2,1,0:T(8,128)(2,1)} async-done(((bf16[6,16,3072]{2,1,0:T(8,128)(2,1)}), bf16[96,16,3072]{2,1,0:T(8,128)(2,1)}) %all-gather.5.cloned.1.call-update) | async-done | bytes 9437200 | tf_op jit(solution)/shard_map/all_gather | solution.py:457
  142.8 7.0 %combine.2.refs_0_ = bf16[6,16,4096]{2,1,0:T(8,128)(2,1)} custom-call(bf16[96,1536]{1,0:T(8,128)(2,1)} %mul.42.weight_ref, bf16[96,16,3072]{2,1,0:T(8,128)(2,1)} %all-gather.5.cloned.1.call-done.field_ref), custom_call_target="tpu_custom_call" | custom-call | flops 56623104 | bytes 9437184 | tf_op jit(solution)/shard_map/combine/pallas_call | solution.py:413
  149.8 68.5 %all-gather.3.cloned.1.call-done.field_ref = bf16[96,16,1024]{2,1,0:T(8,128)(2,1)} async-done(((bf16[6,16,1024]{2,1,0:T(8,128)(2,1)}), bf16[96,16,1024]{2,1,0:T(8,128)(2,1)}) %all-gather.3.cloned.1.call-update) | async-done | bytes 3145744 | tf_op jit(solution)/shard_map/all_gather | solution.py:457
  218.3 3.0 %combine.3 = bf16[6,16,4096]{2,1,0:T(8,128)(2,1)} custom-call(bf16[96,1536]{1,0:T(8,128)(2,1)} %mul.42.weight_ref, bf16[96,16,1024]{2,1,0:T(8,128)(2,1)} %all-gather.3.cloned.1.call-done.field_ref, bf16[6,16,4096]{2,1,0:T(8,128)(2,1)} %combine.2.refs_0_), custom_call_target="tpu_custom_call", output_to_operand_aliasing={{}: (2, {})} | custom-call | flops 18874368 | bytes 3145728 | tf_op jit(solution)/shard_map/combine/pallas_call | solution.py:413
  (8 shorter events, 0.1 us)
Async XLA Ops:
  7.2 135.6 %all-gather.5.cloned.1.call-start = ((), (), s32[]{:S(2)}) async-start(), calls=%async_computation.2 | async-start | bytes 10027008 | tf_op jit(solution)/shard_map/all_gather | solution.py:457
  9.2 209.1 %all-gather.3.cloned.1.call-start = ((), (), s32[]{:S(2)}) async-start(), calls=%async_computation.1 | async-start | bytes 3342336 | tf_op jit(solution)/shard_map/all_gather | solution.py:457
  83.7 20.3 %copy-start = (f32[16,2,8,128]{3,2,1,0:T(8,128)S(1)}, f32[16,2,8,128]{3,2,1,0:T(8,128)}, u32[]{:S(2)}) copy-start(f32[16,2,8,128]{3,2,1,0:T(8,128)} %get-tuple-element.5) | copy-start | bytes 393220
  105.1 18.2 %all-to-all-start = ((f32[16,6,2,128]{3,2,1,0:T(2,128)}), f32[16,6,2,128]{3,2,1,0:T(2,128)S(1)}, u32[]{:S(2)}, u32[]{:S(2)}) async-start(f32[16,6,2,128]{3,2,1,0:T(2,128)} %copy.31), calls=%async_computation | async-start | bytes 196608 | tf_op jit(solution)/shard_map/all_to_all | solution.py:483
Sparse Core Ops, SparseCore 0:
  10.6 132.1 all-gather.4
  144.9 73.3 all-gather.2
where the time goes:
time: 229 us; the launch traced here: 228 us
  waiting for transfers between devices  97.2 us (42%)
  Pallas kernels  78.9 us (34%)
  other arithmetic  18.1 us (8%)
  local copies, waits for them, and re-layouts  15.4 us (7%)
  between operations  14.2 us (6%)
  starting transfers between devices  3.59 us (2%)
    all_gather x2, waiting for transfers between devices, shards(): gathered.append((first, lax.all_gather(piece, 'mem', axis=0, tiled=True)))  87.2 us
    pallas_call x1, Pallas kernels, gram_of_all(): pl.pallas_call(functools.partial(gram_kernel, tiles, planes, local_member...  68.9 us
    pallas_call x2, Pallas kernels, combine(): pl.pallas_call(combine_kernel, grid=(part // width,), in_specs=ins, out_s...  9.99 us
    all_to_all x1, waiting for transfers between devices, shards(): lax.all_to_all(moved.reshape(planes, local, comps, LANES), 'mem', split_a...  9.88 us
    another operation x3, other arithmetic, ensemble_weights(): factor = jnp.linalg.cholesky(identity + gram_matrix)  9.45 us
    another operation x2, other arithmetic, ensemble_weights(): lax.linalg.triangular_solve(factor, identity, left_side=True, lower=True,...  8.01 us
  transfers between devices with their start and end apart: 3, of which 3 were waited for; matrix products, arithmetic and copies ran while one was open for 14% of the time, Pallas kernels for 33%

commit v1 on v0

--- a/solution.py
+++ b/solution.py
@@ -11,6 +11,7 @@
 LANES = 128
 LOW = 256
 STEP = 0.2
+PLAN = (0, 2, 14, 17, 21, 25, 28, 31, 34, 38, 40)
 MESH = pl.DeviceIdType.MESH
 HIGHEST = lax.Precision.HIGHEST
 BF = jnp.bfloat16
@@ -50,18 +51,24 @@
     )
 
 
-def gram_kernel(
+PIECES = 8
+LEAD = 5
+
+
+def assimilation_kernel(
     tiles,
     planes,
-    local_members,
+    local,
     dest_ref,
     cell_ref,
     frac_ref,
     obs_ref,
     sd_ref,
-    table_ref,
-    all_out,
-    gram_out,
+    velocity_ref,
+    velocity_out,
+    positions_out,
+    field,
+    table,
     slot_ref,
     req,
     asked,
@@ -75,6 +82,13 @@
     gpart,
     gplane,
     gall,
+    gfull,
+    weight_t,
+    kron,
+    acc,
+    psend,
+    pall,
+    load_sem,
     send_a,
     send_b,
     send_z,
@@ -82,13 +96,29 @@
     recv_b,
     recv_c,
     recv_e,
+    recv_g,
+    ring_send,
+    ring_recv,
 ):
     me = lax.axis_index("tile")
     mz = lax.axis_index("mem")
     drifters = dest_ref.shape[1]
     width = min(256, drifters)
-    members = planes * local_members
+    members = planes * local
     rows = planes * 8
+    layers = velocity_ref.shape[1]
+    piece = velocity_ref.shape[2] // PIECES
+    inner = local * layers
+    reach = planes // 2
+    slots = PIECES * (reach - 1) + PIECES // 2
+
+    def own_piece(q):
+        return pltpu.make_async_copy(
+            velocity_ref.at[:, :, pl.ds(q * piece, piece)], field.at[mz, q], load_sem.at[q]
+        )
+
+    for q in range(PIECES):
+        own_piece(q).start()
 
     barrier = pltpu.get_barrier_semaphore()
 
@@ -106,6 +136,92 @@
 
     lax.fori_loop(1, tiles, greet_tile, 0)
     lax.fori_loop(1, planes, greet_mem, 0)
+    for q in range(PIECES):
+        own_piece(q).wait()
+    pl.semaphore_wait(barrier, tiles + planes - 2)
+
+    up = lax.rem(mz + 1, planes)
+    down = lax.rem(mz + planes - 1, planes)
+
+    def ring_copy(way, n, source, peer):
+        q = lax.rem(n + way * (PIECES // 2), PIECES)
+        return remote(
+            field.at[source, q],
+            field.at[source, q],
+            ring_send.at[way, lax.rem(n, PIECES)],
+            ring_recv.at[way, n],
+            "mem",
+            peer,
+        )
+
+    def ring_out(way, n):
+        back = n // PIECES
+        source = lax.rem(mz + planes - back, planes) if way == 0 else lax.rem(mz + back, planes)
+        return ring_copy(way, n, source, up if way == 0 else down)
+
+    def ring_source(way, n):
+        back = n // PIECES + 1
+        return lax.rem(mz + planes - back, planes) if way == 0 else lax.rem(mz + back, planes)
+
+    def ring_in(way, n):
+        return ring_copy(way, n, ring_source(way, n), up if way == 0 else down)
+
+    def issue(n):
+        for way in range(2):
+            ring_out(way, n).start()
+
+    def pump(n):
+        for way in range(2):
+            ring_in(way, n).wait_recv()
+        ahead = n + LEAD
+
+        @pl.when(ahead < slots)
+        def _():
+            @pl.when(ahead >= PIECES)
+            def _():
+                for way in range(2):
+                    ring_out(way, ahead - PIECES).wait_send()
+
+            issue(ahead)
+
+    def pumps(first, last):
+        first, last = min(first, slots - 4), min(last, slots - 4)
+        if last > first:
+
+            def one(n, carry):
+                pump(n)
+                return carry
+
+            lax.fori_loop(first, last, one, 0)
+
+    def pumps_in_loop(first, last, i, steps):
+        first, last = min(first, slots - 4), min(last, slots - 4)
+        count = last - first
+        if count > 0:
+
+            def one(n, carry):
+                pump(n)
+                return carry
+
+            lax.fori_loop(first + i * count // steps, first + (i + 1) * count // steps, one, 0)
+
+    for n in range(min(LEAD, slots)):
+        issue(n)
+
+    pick_row = lax.broadcasted_iota(jnp.int32, (16, inner), 0)
+    pick_column = lax.broadcasted_iota(jnp.int32, (16, inner), 1)
+    half = layers // 2
+    pick = ((pick_column // layers) == (pick_row & 7)) & (
+        (pick_column % layers) == half * (pick_row >> 3)
+    )
+    pick = pick.astype(F32).astype(BF)
+    for q in range(PIECES):
+        level = jnp.dot(
+            pick, field[mz, q].reshape(inner, piece), preferred_element_type=F32
+        ).astype(BF)
+        for h in range(piece // LOW):
+            first = (q * (piece // LOW) + h) * 16
+            table[first : first + 16, :] = level[:, LOW * h : LOW * (h + 1)]
 
     tile_row = lax.broadcasted_iota(jnp.int32, (tiles, width), 0)
     earlier = (
@@ -138,8 +254,6 @@
         total = total + nt_dot(spread, hot_slot)
     req[...] = total.reshape(tiles, 8, LANES)
 
-    pl.semaphore_wait(barrier, tiles + planes - 2)
-
     def ask(i, carry):
         peer = lax.rem(me + i, tiles)
         remote(
@@ -149,6 +263,8 @@
 
     lax.fori_loop(1, tiles, ask, 0)
     asked[me] = req[me]
+
+    pumps(PLAN[0], PLAN[1])
 
     def serve(i, carry):
         src = lax.rem(me + tiles - i, tiles)
@@ -173,9 +289,9 @@
         high4 = jnp.concatenate(highs, axis=1)
         cell_row = lax.broadcasted_iota(jnp.int32, (LOW, 4 * LANES), 0).astype(F32)
         hot = (cell_row == low4).astype(F32).astype(BF)
-        found = jnp.dot(table_ref[...], hot, preferred_element_type=F32)
+        found = jnp.dot(table[...], hot, preferred_element_type=F32)
         picked = found[0:16]
-        for h in range(1, table_ref.shape[0] // 16):
+        for h in range(1, table.shape[0] // 16):
             picked = jnp.where(high4 == float(h), found[16 * h : 16 * h + 16], picked)
         corner_x = [picked[0:8, LANES * q : LANES * (q + 1)] for q in range(4)]
         corner_y = [picked[8:16, LANES * q : LANES * (q + 1)] for q in range(4)]
@@ -202,6 +318,8 @@
             ret[src, 0] = x
             ret[src, 1] = y
 
+        pumps_in_loop(PLAN[1], PLAN[2], i, tiles)
+
         return carry
 
     lax.fori_loop(0, tiles, serve, 0)
@@ -214,6 +332,8 @@
         return carry
 
     lax.fori_loop(1, tiles, asked_sent, 0)
+
+    pumps(PLAN[2], PLAN[3])
 
     def returned(i, carry):
         peer = lax.rem(me + i, tiles)
@@ -241,6 +361,7 @@
         for s in range(shares):
             zsend[i * shares + s, 0] = picked[0:8, LANES * s : LANES * (s + 1)]
             zsend[i * shares + s, 1] = picked[8:16, LANES * s : LANES * (s + 1)]
+        pumps_in_loop(PLAN[3], PLAN[4], i, drifters // width)
         return carry
 
     lax.fori_loop(0, drifters // width, order, 0)
@@ -252,6 +373,7 @@
 
     lax.fori_loop(1, planes, share, 0)
     zall[mz] = zsend[mz]
+    pumps(PLAN[4], PLAN[5])
 
     def shared(i, carry):
         peer = lax.rem(mz + i, planes)
@@ -263,7 +385,7 @@
     lax.fori_loop(1, planes, shared, 0)
 
     row = lax.broadcasted_iota(jnp.int32, (rows, LANES), 0)
-    real = (row & 7) < local_members
+    real = (row & 7) < local
     own = pl.ds(pl.multiple_of(mz * LANES, LANES), LANES)
     sd = sd_ref[:, own]
     inverse_scale = 1.0 / (sd * jnp.sqrt(jnp.full(sd.shape, members - 1, F32)))
@@ -273,7 +395,7 @@
         mean = jnp.sum(jnp.where(real, p, 0.0), axis=0, keepdims=True) * (1.0 / members)
         anomaly = jnp.where(real, (p - mean) * inverse_scale, 0.0)
         innovation = (obs_ref[c : c + 1, own] - mean) / sd
-        left = jnp.where(row == local_members, innovation, anomaly)
+        left = jnp.where(row == local, innovation, anomaly)
         gram = gram + nt_dot(left, anomaly, HIGHEST)
     chunk = rows // tiles
     for t in range(tiles):
@@ -286,6 +408,7 @@
 
     lax.fori_loop(1, tiles, scatter, 0)
     grecv[me] = gsend[me]
+    pumps(PLAN[5], PLAN[6])
 
     def scattered(i, carry):
         peer = lax.rem(me + i, tiles)
@@ -309,6 +432,7 @@
 
     lax.fori_loop(1, planes, plane, 0)
     gplane[mz] = partial
+    pumps(PLAN[6], PLAN[7])
 
     def planed(i, carry):
         peer = lax.rem(mz + i, planes)
@@ -330,6 +454,7 @@
 
     lax.fori_loop(1, tiles, gather, 0)
     gall[me] = summed
+    pumps(PLAN[7], PLAN[8])
 
     def gathered(i, carry):
         peer = lax.rem(me + i, tiles)
@@ -339,31 +464,172 @@
         return carry
 
     lax.fori_loop(1, tiles, gathered, 0)
-    all_out[...] = zall[...]
-    gram_out[...] = gall[...]
-
-
-def gram_of_all(tiles, planes, local_members, dest, cell, frac, obs, sd, table):
+
+    for t in range(tiles):
+        gfull[chunk * t : chunk * (t + 1), :] = gall[t]
+    proj_row = gfull[local : local + 1, :]
+    square_row = lax.broadcasted_iota(jnp.int32, (rows, rows), 0)
+    square_column = lax.broadcasted_iota(jnp.int32, (rows, rows), 1)
+    one = (square_row == square_column).astype(F32)
+    left = jnp.where((square_row & 7) < local, gfull[...], 0.0) + one
+    inverse = one
+    for b in range(planes):
+        height = rows - 8 * b
+        step_row = lax.broadcasted_iota(jnp.int32, (height, rows), 0)
+        for r in range(local):
+            k = 8 * b + r
+            pivot = left[r : r + 1, k : k + 1]
+            scale = lax.rsqrt(pivot)
+            scale = scale * (1.5 - 0.5 * pivot * scale * scale)
+            left_row = left[r : r + 1] * scale
+            inverse_row = inverse[r : r + 1] * scale
+            column = jnp.where(step_row > r, left[:, k : k + 1] * scale, 0.0)
+            left = left - column * left_row
+            inverse = jnp.where(step_row == r, inverse_row, inverse - column * inverse_row)
+        weight_t[8 * b : 8 * b + 8, :] = inverse[0:8]
+        if b + 1 < planes:
+            left, inverse = left[8:], inverse[8:]
+        pumps(PLAN[8] + (PLAN[9] - PLAN[8]) * b // planes, PLAN[8] + (PLAN[9] - PLAN[8]) * (b + 1) // planes)
+
+    real_square = ((square_row & 7) < local) & ((square_column & 7) < local)
+    root = jnp.where(real_square, weight_t[...], 0.0)
+    solved = jnp.sum(root * proj_row, axis=1, keepdims=True)
+    mean_weight = jnp.sum(root * solved, axis=0, keepdims=True)
+    grown = mean_weight + jnp.sqrt(jnp.full((rows, rows), members - 1, F32)) * root
+    grown = jnp.where(real_square, grown, 0.0)
+    centre = jnp.sum(grown, axis=1, keepdims=True) * (1.0 / members)
+    weights = jnp.where(real_square, grown - centre + 1.0 / members, 0.0)
+    weight_t[...] = weights
+
+    for c in range(2):
+        share_of = zall[:, c].reshape(rows, LANES)
+        share_of = jnp.where(real, share_of, 0.0)
+        moved = jnp.dot(weights, share_of, precision=HIGHEST, preferred_element_type=F32)
+        psend[:, c] = moved.reshape(planes, 8, LANES)
+
+    def give(i, carry):
+        peer = lax.rem(mz + i, planes)
+        remote(psend.at[peer], pall.at[mz], send_z.at[peer], recv_g.at[mz], "mem", peer).start()
+        return carry
+
+    lax.fori_loop(1, planes, give, 0)
+    pall[mz] = psend[mz]
+    pumps(PLAN[9], PLAN[10])
+
+    own_weights = weight_t[pl.ds(pl.multiple_of(mz * 8, 8), 8), :].astype(BF)
+    up_row = lax.broadcasted_iota(jnp.int32, (inner, 8), 0)
+    up_column = lax.broadcasted_iota(jnp.int32, (inner, 8), 1)
+    tall = jnp.dot(
+        ((up_row // layers) == up_column).astype(F32).astype(BF),
+        own_weights,
+        preferred_element_type=F32,
+    ).astype(BF)
+    for z in range(planes):
+        wide_row = lax.broadcasted_iota(jnp.int32, (rows, 8 * layers), 0)
+        wide_column = lax.broadcasted_iota(jnp.int32, (rows, 8 * layers), 1)
+        spread = jnp.dot(
+            tall,
+            (wide_row == 8 * z + wide_column // layers).astype(F32).astype(BF),
+            preferred_element_type=F32,
+        )
+        same = (lax.broadcasted_iota(jnp.int32, (inner, 8 * layers), 0) % layers) == (
+            lax.broadcasted_iota(jnp.int32, (inner, 8 * layers), 1) % layers
+        )
+        kron[z] = jnp.where(same, spread, 0.0).astype(BF)
+
+    def term(source, q):
+        block = field[source, q].reshape(inner, piece)
+        return jnp.dot(kron[source][:, :inner], block, preferred_element_type=F32)
+
+    def own_term(q, carry):
+        acc[q] = term(mz, q)
+        return carry
+
+    lax.fori_loop(0, PIECES, own_term, 0)
+
+    def add_slot(n):
+        for way in range(2):
+            q = lax.rem(n + way * (PIECES // 2), PIECES)
+            acc[q] = acc[q] + term(ring_source(way, n), q)
+
+    begin = min(PLAN[10], slots - 4)
+    rest = slots - begin - 2
+
+    def follow(n, carry):
+        pump(n)
+        j = n - begin
+
+        def late(s, carry):
+            add_slot(s)
+            return carry
+
+        lax.fori_loop(
+            jnp.minimum(j * begin // rest, begin), jnp.minimum((j + 1) * begin // rest, begin), late, 0
+        )
+        add_slot(n)
+        return carry
+
+    lax.fori_loop(begin, slots, follow, 0)
+    for q in range(PIECES):
+        velocity_out[:, :, piece * q : piece * (q + 1)] = (
+            acc[q].astype(BF).reshape(local, layers, piece)
+        )
+
+    def given(i, carry):
+        peer = lax.rem(mz + i, planes)
+        copy = remote(psend.at[peer], pall.at[peer], send_z.at[peer], recv_g.at[peer], "mem", peer)
+        copy.wait_send()
+        copy.wait_recv()
+        return carry
+
+    lax.fori_loop(1, planes, given, 0)
+
+    def place(z, carry):
+        lanes = pl.ds(pl.multiple_of(z * LANES, LANES), LANES)
+        for c in range(2):
+            block = pall[z, c]
+            for m in range(local):
+                positions_out[m, c : c + 1, lanes] = block[m : m + 1]
+        return carry
+
+    lax.fori_loop(0, planes, place, 0)
+    for n in range(max(slots - PIECES, 0), slots):
+        for way in range(2):
+            ring_out(way, n).wait_send()
+
+
+def shards(velocity, start_frac, observed, obs_sd, tile_of, cell_of):
+    local, comps, levels, cells = velocity.shape
+    tiles = lax.axis_size("tile")
+    planes = lax.axis_size("mem")
+    drifters = cell_of.shape[0]
+    layers = comps * levels
     rows = planes * 8
     chunk = rows // tiles
+    inner = local * layers
+    piece = cells // PIECES
+    slots = PIECES * (planes // 2 - 1) + PIECES // 2
     vmem = pl.BlockSpec(memory_space=pltpu.VMEM)
     dma = pltpu.SemaphoreType.DMA
     f32 = lambda *shape: pltpu.VMEM(shape, F32)
-    return pl.pallas_call(
-        functools.partial(gram_kernel, tiles, planes, local_members),
+    bf16 = lambda *shape: pltpu.VMEM(shape, BF)
+    new_velocity, new_positions = pl.pallas_call(
+        functools.partial(assimilation_kernel, tiles, planes, local),
         out_shape=(
-            jax.ShapeDtypeStruct((planes, 2, 8, LANES), F32),
-            jax.ShapeDtypeStruct((tiles, chunk, rows), F32),
+            jax.ShapeDtypeStruct((local, layers, cells), BF),
+            jax.ShapeDtypeStruct((local, comps, drifters), F32),
         ),
-        in_specs=[vmem] * 6,
+        in_specs=[vmem] * 5 + [pl.BlockSpec(memory_space=pl.ANY)],
         out_specs=(vmem, vmem),
         scratch_shapes=[
-            f32(1, dest.shape[1]),
+            bf16(planes, PIECES, local, layers, piece),
+            bf16(cells // LOW * 16, LOW),
+            f32(1, drifters),
             f32(tiles, 8, LANES),
             f32(tiles, 8, LANES),
             f32(tiles, 2, 8, LANES),
             f32(tiles, 2, 8, LANES),
-            pltpu.VMEM((tiles * 16, 3 * LANES), BF),
+            bf16(tiles * 16, 3 * LANES),
             f32(planes, 2, 8, LANES),
             f32(planes, 2, 8, LANES),
             f32(tiles, chunk, rows),
@@ -371,6 +637,13 @@
             f32(chunk, rows),
             f32(planes, chunk, rows),
             f32(tiles, chunk, rows),
+            f32(rows, rows),
+            f32(rows, rows),
+            bf16(planes, inner, 8 * layers),
+            f32(PIECES, inner, piece),
+            f32(planes, 2, 8, LANES),
+            f32(planes, 2, 8, LANES),
+            dma((PIECES,)),
             dma((tiles,)),
             dma((tiles,)),
             dma((planes,)),
@@ -378,122 +651,23 @@
             dma((tiles,)),
             dma((planes,)),
             dma((planes,)),
+            dma((planes,)),
+            dma((2, PIECES)),
+            dma((2, slots)),
         ],
-        compiler_params=pltpu.CompilerParams(collective_id=0, has_side_effects=True),
-        cost_estimate=pl.CostEstimate(
-            flops=100_000_000_000, bytes_accessed=4_000_000, transcendentals=0
+        compiler_params=pltpu.CompilerParams(
+            collective_id=0, has_side_effects=True, vmem_limit_bytes=56 << 20
         ),
-        name="gram",
-    )(dest, cell, frac, obs, sd, table)
-
-
-def combine_kernel(weight_ref, field_ref, *refs):
-    out_ref = refs[-1]
-    rows = weight_ref.shape[1]
-    width = field_ref.shape[2]
-    field = field_ref[...].reshape(rows, width)
-    out = jnp.dot(weight_ref[...], field, preferred_element_type=F32)
-    out_ref[...] = out.astype(BF).reshape(out_ref.shape)
-
-
-def combine(kron, gathered, first, cells, width, so_far):
-    members, layers, part = gathered.shape
-    local = kron.shape[0] // layers
-    start = first // width
-    ins = [
-        pl.BlockSpec(kron.shape, lambda i: (0, 0)),
-        pl.BlockSpec((members, layers, width), lambda i: (0, 0, i)),
-    ]
-    args = [kron, gathered]
-    alias = {}
-    if so_far is not None:
-        ins.append(pl.BlockSpec(memory_space=pl.ANY))
-        args.append(so_far)
-        alias = {2: 0}
-    return pl.pallas_call(
-        combine_kernel,
-        grid=(part // width,),
-        in_specs=ins,
-        out_specs=pl.BlockSpec((local, layers, width), lambda i: (0, 0, start + i)),
-        out_shape=jax.ShapeDtypeStruct((local, layers, cells), BF),
-        input_output_aliases=alias,
-        cost_estimate=pl.CostEstimate(
-            flops=2 * members * local * layers * part,
-            bytes_accessed=2 * members * layers * part,
-            transcendentals=0,
-        ),
-        name="combine",
-    )(*args)
-
-
-def ensemble_weights(gram_matrix, projection):
-    members = gram_matrix.shape[0]
-    identity = jnp.eye(members, dtype=jnp.float32)
-    factor = jnp.linalg.cholesky(identity + gram_matrix)
-    inverse_root = lax.linalg.triangular_solve(
-        factor, identity, left_side=True, lower=True, transpose_a=True
-    )
-    half_solve = jnp.dot(projection[None], inverse_root, precision=HIGHEST)
-    mean_weight = jnp.sum(inverse_root * half_solve, axis=1, keepdims=True)
-    combined = mean_weight + jnp.sqrt(jnp.float32(members - 1)) * inverse_root
-    return combined - jnp.mean(combined, axis=0, keepdims=True) + 1.0 / members
-
-
-CHUNKS = (3072, 1024)
-
-
-def shards(velocity, start_frac, observed, obs_sd, tile_of, cell_of):
-    local, comps, levels, cells = velocity.shape
-    tiles = lax.axis_size("tile")
-    planes = lax.axis_size("mem")
-    members = planes * local
-    drifters = cell_of.shape[0]
-    layers = comps * levels
-
-    field = velocity.reshape(local, layers, cells)
-    gathered, first = [], 0
-    for size in CHUNKS:
-        piece = lax.slice_in_dim(field, first, first + size, axis=2)
-        gathered.append((first, lax.all_gather(piece, "mem", axis=0, tiled=True)))
-        first += size
-
-    table = velocity[:, :, 0, :].reshape(local, comps, cells // LOW, LOW)
-    table = jnp.pad(table.transpose(2, 1, 0, 3), ((0, 0), (0, 0), (0, 8 - local), (0, 0)))
-    table = table.reshape(-1, LOW)
-    predicted, gram = gram_of_all(
-        tiles,
-        planes,
-        local,
+        name="assimilation",
+    )(
         tile_of.reshape(1, drifters),
         cell_of.reshape(1, drifters),
         start_frac,
         observed,
         obs_sd.reshape(1, drifters),
-        table,
+        velocity.reshape(local, layers, cells),
     )
-    gram = gram.reshape(planes, 8, planes, 8)
-    projection = gram[0, local, :, :local].reshape(members)
-    gram_matrix = gram[:, :local, :, :local].reshape(members, members)
-    weights = ensemble_weights(gram_matrix, projection)
-
-    everyone = predicted[:, :, :local]
-    moved = jnp.einsum(
-        "zmn,zcmp->ncp", weights.reshape(planes, local, members), everyone, precision=HIGHEST
-    )
-    moved = lax.all_to_all(
-        moved.reshape(planes, local, comps, LANES), "mem", split_axis=0, concat_axis=0, tiled=True
-    )
-    new_positions = moved.transpose(1, 2, 0, 3).reshape(local, comps, drifters)
-
-    first_member = lax.axis_index("mem") * local
-    own_columns = lax.dynamic_slice_in_dim(weights, first_member, local, 1).astype(BF)
-    same = jnp.eye(layers, dtype=BF)
-    kron = own_columns.T[:, None, :, None] * same[None, :, None, :]
-    kron = kron.reshape(local * layers, members * layers)
-    out = None
-    for first, part in gathered:
-        out = combine(kron, part, first, cells, 512, out)
-    return (out.reshape(local, comps, levels, cells), new_positions)
+    return (new_velocity.reshape(velocity.shape), new_positions)
 
 
 def solution(mesh):

time: 229 us -> 171 us (0.75)
  the two profiles are of different devices: /device:TPU:2 before, /device:TPU:1 now
where the time goes in v1:
time: 171 us
  Pallas kernels  167 us (98%)
  local copies, waits for them, and re-layouts  2.74 us (2%)
    pallas_call x1, Pallas kernels, shards(): pl.pallas_call(functools.partial(assimilation_kernel, tiles, planes, loca...  167 us

profile of v1, /device:TPU:1, one launch (start us, length us, event | category | flops | bytes accessed | tf_op | source)
XLA Modules:
  0.0 170.7 jit_solution(10570133463745060163)
XLA Ops:
  0.6 167.3 %assimilation.1 = (bf16[6,16,4096]{2,1,0:T(8,128)(2,1)}, f32[6,2,2048]{2,1,0:T(2,128)}) custom-call(s32[1,2048]{1,0:T(1,128)} %bitcast.7, s32[1,2048]{1,0:T(1,128)} %bitcast.8, f32[2,2048]{1,0:T(2,128)} %frac_ref.1, f32[2,2048]{1,0:T(2,128)} %obs_ref.1, f32[1,2048]{1,0:T(1,128)} %bitcast.9, bf16[6,16,4096]{2,1,0:T(8,128)(2,1)} %bitcast.5), custom_call_target="tpu_custom_call" | custom-call | tf_op jit(solution)/shard_map/assimilation/pallas_call | solution.py:616
  167.9 0.0 copy-start
  167.9 2.1 %copy.10 = bf16[6,2,8,4096]{3,2,1,0:T(8,128)(2,1)} copy(bf16[6,2,8,4096]{3,2,1,0:T(8,128)(2,1)} %bitcast.6) | data formatting | bytes 1572864
  170.0 0.0 copy-done
  170.0 0.6 copy.11
Async XLA Ops:
  167.9 2.1 %copy-start = (f32[6,2,2048]{2,1,0:T(2,128)S(1)}, f32[6,2,2048]{2,1,0:T(2,128)}, u32[]{:S(2)}) copy-start(f32[6,2,2048]{2,1,0:T(2,128)} %get-tuple-element.9) | copy-start | bytes 294916

commit v2 on v1

--- a/solution.py
+++ b/solution.py
@@ -53,6 +53,7 @@
 
 PIECES = 8
 LEAD = 5
+UP = 4
 
 
 def assimilation_kernel(
@@ -77,6 +78,7 @@
     parts,
     zsend,
     zall,
+    zpad,
     gsend,
     grecv,
     gpart,
@@ -86,6 +88,7 @@
     weight_t,
     kron,
     acc,
+    pstage,
     psend,
     pall,
     load_sem,
@@ -110,7 +113,9 @@
     piece = velocity_ref.shape[2] // PIECES
     inner = local * layers
     reach = planes // 2
-    slots = PIECES * (reach - 1) + PIECES // 2
+    base = PIECES * (reach - 1)
+    slots = (base + UP, base + PIECES - UP)
+    shift = (0, UP)
 
     def own_piece(q):
         return pltpu.make_async_copy(
@@ -120,6 +125,8 @@
     for q in range(PIECES):
         own_piece(q).start()
 
+    up = lax.rem(mz + 1, planes)
+    down = lax.rem(mz + planes - 1, planes)
     barrier = pltpu.get_barrier_semaphore()
 
     def greet_tile(i, carry):
@@ -128,23 +135,21 @@
         )
         return carry
 
+    lax.fori_loop(1, tiles, greet_tile, 0)
+
     def greet_mem(i, carry):
         pl.semaphore_signal(
             barrier, inc=1, device_id={"mem": lax.rem(mz + i, planes)}, device_id_type=MESH
         )
         return carry
 
-    lax.fori_loop(1, tiles, greet_tile, 0)
     lax.fori_loop(1, planes, greet_mem, 0)
     for q in range(PIECES):
         own_piece(q).wait()
     pl.semaphore_wait(barrier, tiles + planes - 2)
 
-    up = lax.rem(mz + 1, planes)
-    down = lax.rem(mz + planes - 1, planes)
-
     def ring_copy(way, n, source, peer):
-        q = lax.rem(n + way * (PIECES // 2), PIECES)
+        q = lax.rem(n + shift[way], PIECES)
         return remote(
             field.at[source, q],
             field.at[source, q],
@@ -166,26 +171,21 @@
     def ring_in(way, n):
         return ring_copy(way, n, ring_source(way, n), up if way == 0 else down)
 
-    def issue(n):
-        for way in range(2):
-            ring_out(way, n).start()
-
-    def pump(n):
-        for way in range(2):
+    def pump(n, ways=(0, 1)):
+        ahead = n + LEAD
+        for way in ways:
             ring_in(way, n).wait_recv()
-        ahead = n + LEAD
-
-        @pl.when(ahead < slots)
-        def _():
-            @pl.when(ahead >= PIECES)
+
+            @pl.when(ahead < slots[way])
             def _():
-                for way in range(2):
+                @pl.when(ahead >= PIECES)
+                def _():
                     ring_out(way, ahead - PIECES).wait_send()
 
-            issue(ahead)
+                ring_out(way, ahead).start()
 
     def pumps(first, last):
-        first, last = min(first, slots - 4), min(last, slots - 4)
+        first, last = min(first, base - 4), min(last, base - 4)
         if last > first:
 
             def one(n, carry):
@@ -195,7 +195,7 @@
             lax.fori_loop(first, last, one, 0)
 
     def pumps_in_loop(first, last, i, steps):
-        first, last = min(first, slots - 4), min(last, slots - 4)
+        first, last = min(first, base - 4), min(last, base - 4)
         count = last - first
         if count > 0:
 
@@ -205,8 +205,9 @@
 
             lax.fori_loop(first + i * count // steps, first + (i + 1) * count // steps, one, 0)
 
-    for n in range(min(LEAD, slots)):
-        issue(n)
+    for n in range(LEAD):
+        for way in range(2):
+            ring_out(way, n).start()
 
     pick_row = lax.broadcasted_iota(jnp.int32, (16, inner), 0)
     pick_column = lax.broadcasted_iota(jnp.int32, (16, inner), 1)
@@ -359,8 +360,9 @@
         for t in range(1, tiles):
             picked = jnp.where(dest == t, found[16 * t : 16 * t + 16], picked)
         for s in range(shares):
-            zsend[i * shares + s, 0] = picked[0:8, LANES * s : LANES * (s + 1)]
-            zsend[i * shares + s, 1] = picked[8:16, LANES * s : LANES * (s + 1)]
+            lanes_of = slice(LANES * s, LANES * (s + 1))
+            zsend[i * shares + s, 0:local] = picked[0:local, lanes_of]
+            zsend[i * shares + s, local : 2 * local] = picked[8 : 8 + local, lanes_of]
         pumps_in_loop(PLAN[3], PLAN[4], i, drifters // width)
         return carry
 
@@ -383,6 +385,9 @@
         return carry
 
     lax.fori_loop(1, planes, shared, 0)
+
+    for c in range(2):
+        zpad[:, c, 0:local] = zall[:, c * local : (c + 1) * local]
 
     row = lax.broadcasted_iota(jnp.int32, (rows, LANES), 0)
     real = (row & 7) < local
@@ -391,7 +396,7 @@
     inverse_scale = 1.0 / (sd * jnp.sqrt(jnp.full(sd.shape, members - 1, F32)))
     gram = jnp.zeros((rows, rows), F32)
     for c in range(2):
-        p = zall[:, c].reshape(rows, LANES)
+        p = zpad[:, c].reshape(rows, LANES)
         mean = jnp.sum(jnp.where(real, p, 0.0), axis=0, keepdims=True) * (1.0 / members)
         anomaly = jnp.where(real, (p - mean) * inverse_scale, 0.0)
         innovation = (obs_ref[c : c + 1, own] - mean) / sd
@@ -502,10 +507,11 @@
     weight_t[...] = weights
 
     for c in range(2):
-        share_of = zall[:, c].reshape(rows, LANES)
+        share_of = zpad[:, c].reshape(rows, LANES)
         share_of = jnp.where(real, share_of, 0.0)
         moved = jnp.dot(weights, share_of, precision=HIGHEST, preferred_element_type=F32)
-        psend[:, c] = moved.reshape(planes, 8, LANES)
+        pstage[:, c * local : (c + 1) * local] = moved.reshape(planes, 8, LANES)[:, 0:local]
+    psend[...] = pstage[...].astype(BF)
 
     def give(i, carry):
         peer = lax.rem(mz + i, planes)
@@ -549,11 +555,11 @@
 
     def add_slot(n):
         for way in range(2):
-            q = lax.rem(n + way * (PIECES // 2), PIECES)
+            q = lax.rem(n + shift[way], PIECES)
             acc[q] = acc[q] + term(ring_source(way, n), q)
 
-    begin = min(PLAN[10], slots - 4)
-    rest = slots - begin - 2
+    begin = min(PLAN[10], base - 4)
+    rest = base - begin - 1
 
     def follow(n, carry):
         pump(n)
@@ -569,11 +575,7 @@
         add_slot(n)
         return carry
 
-    lax.fori_loop(begin, slots, follow, 0)
-    for q in range(PIECES):
-        velocity_out[:, :, piece * q : piece * (q + 1)] = (
-            acc[q].astype(BF).reshape(local, layers, piece)
-        )
+    lax.fori_loop(begin, base, follow, 0)
 
     def given(i, carry):
         peer = lax.rem(mz + i, planes)
@@ -586,15 +588,25 @@
 
     def place(z, carry):
         lanes = pl.ds(pl.multiple_of(z * LANES, LANES), LANES)
+        block = pall[z].astype(F32)
         for c in range(2):
-            block = pall[z, c]
             for m in range(local):
-                positions_out[m, c : c + 1, lanes] = block[m : m + 1]
+                positions_out[m, c : c + 1, lanes] = block[c * local + m : c * local + m + 1]
         return carry
 
     lax.fori_loop(0, planes, place, 0)
-    for n in range(max(slots - PIECES, 0), slots):
-        for way in range(2):
+
+    for n in range(base, max(slots)):
+        ways = [way for way in range(2) if n < slots[way]]
+        pump(n, ways)
+        for way in ways:
+            q = (n + shift[way]) % PIECES
+            out = acc[q] + term(ring_source(way, n), q)
+            velocity_out[:, :, piece * q : piece * (q + 1)] = (
+                out.astype(BF).reshape(local, layers, piece)
+            )
+    for way in range(2):
+        for n in range(slots[way] - PIECES, slots[way]):
             ring_out(way, n).wait_send()
 
 
@@ -608,7 +620,7 @@
     chunk = rows // tiles
     inner = local * layers
     piece = cells // PIECES
-    slots = PIECES * (planes // 2 - 1) + PIECES // 2
+    slots = PIECES * (planes // 2 - 1) + max(UP, PIECES - UP)
     vmem = pl.BlockSpec(memory_space=pltpu.VMEM)
     dma = pltpu.SemaphoreType.DMA
     f32 = lambda *shape: pltpu.VMEM(shape, F32)
@@ -619,7 +631,7 @@
             jax.ShapeDtypeStruct((local, layers, cells), BF),
             jax.ShapeDtypeStruct((local, comps, drifters), F32),
         ),
-        in_specs=[vmem] * 5 + [pl.BlockSpec(memory_space=pl.ANY)],
+        in_specs=[vmem] * 5 + [pl.BlockSpec(memory_space=pltpu.HBM)],
         out_specs=(vmem, vmem),
         scratch_shapes=[
             bf16(planes, PIECES, local, layers, piece),
@@ -630,7 +642,8 @@
             f32(tiles, 2, 8, LANES),
             f32(tiles, 2, 8, LANES),
             bf16(tiles * 16, 3 * LANES),
-            f32(planes, 2, 8, LANES),
+            f32(planes, 2 * local, LANES),
+            f32(planes, 2 * local, LANES),
             f32(planes, 2, 8, LANES),
             f32(tiles, chunk, rows),
             f32(tiles, chunk, rows),
@@ -641,8 +654,9 @@
             f32(rows, rows),
             bf16(planes, inner, 8 * layers),
             f32(PIECES, inner, piece),
-            f32(planes, 2, 8, LANES),
-            f32(planes, 2, 8, LANES),
+            f32(planes, 2 * local, LANES),
+            bf16(planes, 2 * local, LANES),
+            bf16(planes, 2 * local, LANES),
             dma((PIECES,)),
             dma((tiles,)),
             dma((tiles,)),
@@ -656,7 +670,7 @@
             dma((2, slots)),
         ],
         compiler_params=pltpu.CompilerParams(
-            collective_id=0, has_side_effects=True, vmem_limit_bytes=56 << 20
+            collective_id=0, has_side_effects=True, vmem_limit_bytes=65_700_000
         ),
         name="assimilation",
     )(

time: 171 us -> 165 us (0.965)
  Pallas kernels: 167 us -> 161 us
    pallas_call x1, Pallas kernels: 167 us -> 161 us  [shards(): pl.pallas_call(functools.partial(assimilation_kernel, tiles, planes, loca...]
where the time goes in v2:
time: 165 us; the launch traced here: 164 us
  Pallas kernels  161 us (98%)
  local copies, waits for them, and re-layouts  2.74 us (2%)
    pallas_call x1, Pallas kernels, shards(): pl.pallas_call(functools.partial(assimilation_kernel, tiles, planes, loca...  161 us

profile of v2, /device:TPU:1, one launch (start us, length us, event | category | flops | bytes accessed | tf_op | source)
XLA Modules:
  0.0 164.4 jit_solution(8921090683893799330)
XLA Ops:
  0.6 161.0 %assimilation.1 = (bf16[6,16,4096]{2,1,0:T(8,128)(2,1)}, f32[6,2,2048]{2,1,0:T(2,128)}) custom-call(s32[1,2048]{1,0:T(1,128)} %bitcast.7, s32[1,2048]{1,0:T(1,128)} %bitcast.8, f32[2,2048]{1,0:T(2,128)} %frac_ref.1, f32[2,2048]{1,0:T(2,128)} %obs_ref.1, f32[1,2048]{1,0:T(1,128)} %bitcast.9, bf16[6,16,4096]{2,1,0:T(8,128)(2,1)} %bitcast.5), custom_call_target="tpu_custom_call" | custom-call | tf_op jit(solution)/shard_map/assimilation/pallas_call | solution.py:628
  161.7 0.0 copy-start
  161.7 2.1 %copy.10 = bf16[6,2,8,4096]{3,2,1,0:T(8,128)(2,1)} copy(bf16[6,2,8,4096]{3,2,1,0:T(8,128)(2,1)} %bitcast.6) | data formatting | bytes 1572864
  163.8 0.0 copy-done
  163.8 0.6 copy.11
Async XLA Ops:
  161.7 2.1 %copy-start = (f32[6,2,2048]{2,1,0:T(2,128)S(1)}, f32[6,2,2048]{2,1,0:T(2,128)}, u32[]{:S(2)}) copy-start(f32[6,2,2048]{2,1,0:T(2,128)} %get-tuple-element.9) | copy-start | bytes 294916
